TPU v7x, 32 devices: a whole 2x2x4 slice. The times are simulated.
32 devices in a mesh: grp: 8 (over y, x, core), rep: 4 (over z).
Axes of the slice: x: 2, y: 2, z: 4, core: 2. Of those that a mesh axis runs over, the one named last changes fastest.
Arguments:
- momentum: bfloat16 [256, 4096], P(('grp', 'rep')), may hold values from -6 to 6
- picked: int32 [256, 32], P(('grp', 'rep')), may hold values from 0 to 4095, as said below
- owner_span_order: int32 [8], replicated, may hold values from 0 to 7, each once
Outputs:
- update: bfloat16 [8, 4096], replicated
- residual_momentum: bfloat16 [256, 4096], P(('grp', 'rep'))
Inputs may be any that keep to these rules, and one draw needn't show every extreme that they name: `picked`: the 32 numbers of a row are different. `owner_span_order`: each span stands once.
All inputs are finite; a program needn't handle non-finite values.
Results may differ from a plain program's by a relative error of at most 0.013.
Values may be sent and summed in bfloat16 or wider, within the bound.
A program may use at most 64 MiB of HBM per device.

v0:
```python
import math

import jax
import jax.numpy as jnp
from jax import lax
from jax.sharding import PartitionSpec as P

BLOCK = 64
TOPK = 32
CH_OWN = 1


def dct_cosines(points):
    freq = jnp.arange(points, dtype=jnp.float32)[:, None]
    place = jnp.arange(points, dtype=jnp.float32)[None, :]
    values = jnp.cos(jnp.pi * (2.0 * place + 1.0) * freq / (2.0 * points)) * jnp.sqrt(2.0 / points)
    values = values.at[0].multiply(jnp.sqrt(0.5))
    rounded = lax.optimization_barrier(values.astype(jnp.bfloat16))
    return rounded.astype(jnp.float32)


def forward(square_low, cosines, cos_low):
    half = jnp.einsum("cab,jb->caj", square_low, cos_low, preferred_element_type=jnp.float32)
    return jnp.einsum("ia,caj->cij", cosines, half, precision=lax.Precision.HIGHEST)


def decode(dense_matrix, cosines):
    square = dense_matrix.reshape(dense_matrix.shape[0], BLOCK, BLOCK)
    half = jnp.einsum("cij,jb->cib", square, cosines, precision=lax.Precision.HIGHEST)
    full = jnp.einsum("ia,cib->cab", cosines, half, precision=lax.Precision.HIGHEST)
    return full.reshape(dense_matrix.shape[0], BLOCK * BLOCK)


def decode_sparse(dense_low, cosines, cos_low):
    square = dense_low.reshape(dense_low.shape[0], BLOCK, BLOCK)
    half = jnp.einsum("cij,jb->cib", square, cos_low, preferred_element_type=jnp.float32)
    full = jnp.einsum("ia,cib->cab", cosines, half, precision=lax.Precision.HIGHEST)
    return full.reshape(dense_low.shape[0], BLOCK * BLOCK)


def densify(values, spots):
    entries, columns = values.shape
    per_step = math.gcd(entries, max(1, 65536 // columns))
    positions = jnp.arange(BLOCK, dtype=jnp.int32)

    def one_block(pieces):
        block_values, block_spots = pieces
        zeros = jnp.zeros_like(block_values)
        row_onehot = jnp.where(
            (block_spots // BLOCK)[:, None, :] == positions[None, :, None],
            block_values[:, None, :],
            zeros[:, None, :],
        )
        column_onehot = ((block_spots % BLOCK)[:, None, :] == positions[None, :, None]).astype(
            jnp.bfloat16
        )
        dense_matrix = jnp.einsum(
            "bcy,bzy->bcz", row_onehot, column_onehot, preferred_element_type=jnp.float32
        )
        return dense_matrix.reshape(per_step, BLOCK * BLOCK)

    stacked = lax.map(
        one_block,
        (
            values.reshape(entries // per_step, per_step, columns),
            spots.reshape(entries // per_step, per_step, columns),
        ),
    )
    return stacked.reshape(entries, BLOCK * BLOCK)


def owner_sum(received):
    values, spots = received
    return densify(values[0], spots[0])


def local(momentum, picked, owner_span_order):
    cosines = dct_cosines(BLOCK)
    cos_low = cosines.astype(jnp.bfloat16)
    owners = lax.axis_size("grp")
    span_count = momentum.shape[0]
    square_low = momentum.reshape(span_count, BLOCK, BLOCK)
    transform_coefficients = forward(square_low, cosines, cos_low).reshape(
        span_count, BLOCK * BLOCK
    )
    chosen = jnp.take_along_axis(transform_coefficients, picked, axis=1).astype(jnp.bfloat16)
    own_dense = densify(chosen, picked).astype(jnp.bfloat16)
    residual_momentum = (
        momentum.astype(jnp.float32) - decode_sparse(own_dense, cosines, cos_low)
    ).astype(jnp.bfloat16)
    slot_values = jnp.take(chosen, owner_span_order, axis=0)
    slot_spots = jnp.take(picked, owner_span_order, axis=0)
    shaped = (slot_values.reshape(owners, CH_OWN, TOPK), slot_spots.reshape(owners, CH_OWN, TOPK))
    partial_sum = owner_sum(
        (
            lax.all_to_all(shaped[0], "grp", split_axis=0, concat_axis=2, tiled=True),
            lax.all_to_all(shaped[1], "grp", split_axis=0, concat_axis=2, tiled=True),
        )
    )
    partial_sum = lax.psum(partial_sum, "rep")
    my_share = decode(partial_sum, cosines).astype(jnp.bfloat16)
    update = lax.all_gather(my_share, "grp", axis=0, tiled=True)
    return (update, residual_momentum)


def solution(mesh):
    return jax.shard_map(
        local,
        mesh=mesh,
        in_specs=(P(("grp", "rep"), None), P(("grp", "rep"), None), P()),
        out_specs=(P(), P(("grp", "rep"), None)),
        check_vma=False,
    )
```

profile of v0, /device:TPU:0, one launch (start us, length us, event | category | flops | bytes accessed | tf_op | source)
XLA Modules:
  0.0 55.1 jit_solution(13529057157685993092)
XLA Ops:
  0.6 0.7 %compare_and_fusion = pred[8]{0:T(512)(128)(4,1)S(1)} fusion(s32[8]{0:T(128)} %param.7), kind=kLoop, calls=%fused_computation.49 | loop fusion | flops 48 | bytes 40 | tf_op jit(solution)/shard_map/jit(_take)/and | solution.py:91
  1.4 0.6 %copy-done = s32[8,32]{1,0:T(8,128)S(1)} copy-done((s32[8,32]{1,0:T(8,128)S(1)}, s32[8,32]{1,0:T(8,128)}, u32[]{:S(2)}) %copy-start) | copy-done | bytes 1048
  2.1 0.1 cosine_multiply_fusion
  2.4 0.2 reshape.317
  2.5 0.3 convolution_bitcast_fusion.2
  2.8 0.3 convolution_bitcast_fusion.1
  3.1 0.1 copy.19
  3.2 0.2 reshape.318
  3.4 2.4 %gather_fusion.2 = bf16[256]{0:T(256)(128)(2,1)S(1)} fusion(bf16[8,4096]{1,0:T(8,128)(2,1)S(1)} %reshape.318, s32[256]{0:T(256)S(1)} %reshape.340), kind=kCustom, calls=%fused_computation.2 | custom fusion | bytes 3072 | tf_op jit(solution)/shard_map/jit(take_along_axis)/gather | solution.py:86
  5.9 0.6 %gather_fusion.1 = bf16[8,32]{1,0:T(8,128)(2,1)S(1)} fusion(bf16[8,32]{1,0:T(8,128)(2,1)S(1)} %select_convert_fusion, s32[1024]{0:T(1024)S(1)} %pad_clamp_fusion), kind=kCustom, calls=%fused_computation.1 | custom fusion | bytes 1056 | tf_op jit(solution)/shard_map/jit(_take)/gather | solution.py:91
  6.5 0.6 %copy.20 = bf16[8,1,32]{2,1,0:T(2,128)(2,1)} copy(bf16[8,1,32]{2,0,1:T(8,128)(2,1)S(1)} %bitcast_select_fusion.1) | data formatting | bytes 1024 | tf_op jit(solution)/shard_map/jit(_take)/select_n | solution.py:91
  7.1 5.2 %all-to-all-start.1 = ((bf16[8,1,32]{2,1,0:T(2,128)(2,1)}), bf16[8,1,32]{2,1,0:T(2,128)(2,1)S(1)}, u32[]{:S(2)}, u32[]{:S(2)}) async-start(bf16[8,1,32]{2,1,0:T(2,128)(2,1)} %copy.20), calls=%async_computation.1 | async-start | bytes 8192 | tf_op jit(solution)/shard_map/all_to_all | solution.py:96
  12.3 0.6 %gather_fusion = s32[8,32]{1,0:T(8,128)S(1)} fusion(s32[8,32]{1,0:T(8,128)S(1)} %copy-done, s32[1024]{0:T(1024)S(1)} %pad_clamp_fusion), kind=kCustom, calls=%fused_computation | custom fusion | bytes 2080 | tf_op jit(solution)/shard_map/jit(_take)/gather | solution.py:92
  12.9 0.6 %fusion = f32[8,64,64]{1,2,0:T(8,128)S(1)} fusion(s32[8,32]{1,0:T(8,128)S(1)} %get-tuple-element.45, s32[8,32]{1,0:T(8,128)S(1)} %get-tuple-element.44, bf16[8,32]{1,0:T(8,128)(2,1)S(1)} %select_convert_fusion, bf16[64,64]{1,0:T(8,128)(2,1)S(1)} %convert_element_type.42), kind=kOutput, calls=%fused_computation.7 | convolution fusion | flops 6373376 | bytes 141824 | tf_op jit(solution)/shard_map/cij,jb->cib/dot_general | solution.py:36
  13.5 0.3 convolution_bitcast_fusion
  13.8 0.7 %bitcast_select_fusion = s32[8,1,32]{2,0,1:T(8,128)} fusion(s32[8,32]{1,0:T(8,128)S(1)} %gather_fusion, pred[8]{0:T(512)(128)(4,1)S(1)} %compare_and_fusion), kind=kLoop, calls=%fused_computation.40 | loop fusion | flops 256 | bytes 2056 | tf_op jit(solution)/shard_map/jit(_take)/select_n | solution.py:92
  14.4 0.1 copy.23
  14.6 0.1 reshape.322
  14.7 2.3 %all-to-all-done.1 = bf16[8,1,32]{2,1,0:T(2,128)(2,1)S(1)} async-done(((bf16[8,1,32]{2,1,0:T(2,128)(2,1)}), bf16[8,1,32]{2,1,0:T(2,128)(2,1)S(1)}, u32[]{:S(2)}, u32[]{:S(2)}) %all-to-all-start.1) | async-done | bytes 544 | tf_op jit(solution)/shard_map/all_to_all | solution.py:96
  16.9 3.3 %all-to-all-start = ((s32[8,1,32]{2,1,0:T(1,128)}), s32[8,1,32]{2,1,0:T(1,128)S(1)}, u32[]{:S(2)}, u32[]{:S(2)}) async-start(s32[8,1,32]{2,1,0:T(1,128)} %bitcast.1), calls=%async_computation | async-start | bytes 8192 | tf_op jit(solution)/shard_map/all_to_all | solution.py:97
  20.3 0.6 %subtract_convert_fusion = bf16[8,4096]{1,0:T(8,128)(2,1)} fusion(f32[8,4096]{1,0:T(8,128)S(1)} %reshape.322, bf16[8,4096]{1,0:T(8,128)(2,1)S(1)} %copy-done.1), kind=kLoop, calls=%fused_computation.10 | loop fusion | flops 98304 | bytes 262144 | tf_op jit(solution)/shard_map/convert_element_type | solution.py:90
  21.0 3.8 %all-to-all-done = s32[8,1,32]{2,1,0:T(1,128)S(1)} async-done(((s32[8,1,32]{2,1,0:T(1,128)}), s32[8,1,32]{2,1,0:T(1,128)S(1)}, u32[]{:S(2)}, u32[]{:S(2)}) %all-to-all-start) | async-done | bytes 1056 | tf_op jit(solution)/shard_map/all_to_all | solution.py:97
  24.8 0.5 broadcast.298
  25.3 0.7 %reduce.6 = s32[8,32]{1,0:T(8,128)S(1)} reduce(s32[8,1,32]{2,1,0:T(1,128)S(1)} %all-to-all-done, s32[]{:T(128)} %broadcast.298), dimensions={1}, to_apply=%all_to_all.4.reduce_sub_computation.3 | reduce | bytes 2052 | tf_op jit(solution)/shard_map/all_to_all | solution.py:97
  26.1 0.1 fusion.10
  26.2 19.4 %psum.7 = f32[64,64]{1,0:T(8,128)S(1)} all-reduce(f32[64,64]{1,0:T(8,128)S(1)} %fusion.10), channel_id=1, replica_groups=mesh['grp'=8,'rep'=4] {'rep'}, use_global_device_ids=true, to_apply=%region_0.0 | all-reduce | flops 4096 | bytes 32768 | tf_op jit(solution)/shard_map/psum | solution.py:100
  45.6 0.1 fusion.29
  45.7 0.2 fusion.1
  46.0 0.1 copy.21
  46.1 0.1 reshape.353
  46.2 8.3 %all-gather = bf16[8,1,4096]{2,1,0:T(2,128)(2,1)S(1)} all-gather(bf16[1,1,4096]{2,1,0:T(2,128)(2,1)S(1)} %reshape.353), channel_id=1, replica_groups=mesh['grp'=8,'rep'=4] {'grp'}, dimensions={0}, use_global_device_ids=true | all-gather | bytes 73728 | tf_op jit(solution)/shard_map/all_gather | solution.py:102
  54.4 0.7 %copy.27 = bf16[8,1,4096]{2,0,1:T(8,128)(2,1)} copy(bf16[8,1,4096]{2,1,0:T(2,128)(2,1)S(1)} %all-gather) | data formatting | bytes 131072
  (21 shorter events, 0.5 us)
Async XLA Ops:
  0.6 0.7 %copy-start.2 = (s32[8]{0:T(128)S(1)}, s32[8]{0:T(128)}, u32[]{:S(2)}) copy-start(s32[8]{0:T(128)} %param.7) | copy-start | bytes 100
  1.4 0.7 %copy-start = (s32[8,32]{1,0:T(8,128)S(1)}, s32[8,32]{1,0:T(8,128)}, u32[]{:S(2)}) copy-start(s32[8,32]{1,0:T(8,128)} %param.6) | copy-start | bytes 3076
  1.4 1.0 %copy-start.1 = (bf16[8,4096]{1,0:T(8,128)(2,1)S(1)}, bf16[8,4096]{1,0:T(8,128)(2,1)}, u32[]{:S(2)}) copy-start(bf16[8,4096]{1,0:T(8,128)(2,1)} %param.5) | copy-start | bytes 196612
  7.1 9.8 %all-to-all-start.1 = ((bf16[8,1,32]{2,1,0:T(2,128)(2,1)}), bf16[8,1,32]{2,1,0:T(2,128)(2,1)S(1)}, u32[]{:S(2)}, u32[]{:S(2)}) async-start(bf16[8,1,32]{2,1,0:T(2,128)(2,1)} %copy.20), calls=%async_computation.1 | async-start | bytes 8192 | tf_op jit(solution)/shard_map/all_to_all | solution.py:96
  16.9 7.9 %all-to-all-start = ((s32[8,1,32]{2,1,0:T(1,128)}), s32[8,1,32]{2,1,0:T(1,128)S(1)}, u32[]{:S(2)}, u32[]{:S(2)}) async-start(s32[8,1,32]{2,1,0:T(1,128)} %bitcast.1), calls=%async_computation | async-start | bytes 8192 | tf_op jit(solution)/shard_map/all_to_all | solution.py:97
where the time goes:
time: 55.4 us; the launch traced here: 55.1 us
  blocking collectives  27.6 us (50%)
  starting transfers between devices  8.52 us (15%)
  local copies, waits for them, and re-layouts  7.25 us (13%)
  waiting for transfers between devices  6.04 us (11%)
  other arithmetic  3 us (5%)
  matrix products  1.86 us (3%)
  between operations  0.8 us (1%)
    psum x1, blocking collectives, local(): partial_sum = lax.psum(partial_sum, 'rep')  19.4 us
    all_gather x1, blocking collectives, local(): update = lax.all_gather(my_share, 'grp', axis=0, tiled=True)  8.26 us
    all_to_all x1, starting transfers between devices, local(): lax.all_to_all(shaped[0], 'grp', split_axis=0, concat_axis=2, tiled=True)  5.21 us
    all_to_all x1, waiting for transfers between devices, local(): lax.all_to_all(shaped[1], 'grp', split_axis=0, concat_axis=2, tiled=True)  3.79 us
    all_to_all x1, starting transfers between devices, local(): lax.all_to_all(shaped[1], 'grp', split_axis=0, concat_axis=2, tiled=True)  3.31 us
    gather x3, local copies, waits for them, and re-layouts, local(): jnp.take_along_axis(transform_coefficients, picked, axis=1)  2.56 us
    all_to_all x1, waiting for transfers between devices, local(): lax.all_to_all(shaped[0], 'grp', split_axis=0, concat_axis=2, tiled=True)  2.26 us
    unnamed x8, local copies, waits for them, and re-layouts  1.44 us
  transfers between devices with their start and end apart: 2, of which 2 were waited for; matrix products, arithmetic and copies ran while one was open for 6% of the time, Pallas kernels for 0%

commit v1 on v0

--- a/solution.py
+++ b/solution.py
@@ -1,8 +1,13 @@
 import math
+
+import functools
 
 import jax
 import jax.numpy as jnp
+import numpy as np
 from jax import lax
+from jax.experimental import pallas as pl
+from jax.experimental.pallas import tpu as pltpu
 from jax.sharding import PartitionSpec as P
 
 BLOCK = 64
@@ -74,7 +79,7 @@
     return densify(values[0], spots[0])
 
 
-def local(momentum, picked, owner_span_order):
+def local_large(momentum, picked, owner_span_order):
     cosines = dct_cosines(BLOCK)
     cos_low = cosines.astype(jnp.bfloat16)
     owners = lax.axis_size("grp")
@@ -103,9 +108,201 @@
     return (update, residual_momentum)
 
 
+LANES = 128
+GATHER_BYTES = 2**20
+
+
+def cosine_table():
+    freq = np.arange(BLOCK, dtype=np.float64)[:, None]
+    place = np.arange(BLOCK, dtype=np.float64)[None, :]
+    values = np.cos(np.pi * (2 * place + 1) * freq / (2 * BLOCK)) * np.sqrt(2 / BLOCK)
+    values[0] *= np.sqrt(0.5)
+    return values.astype(np.float32)
+
+
+def contract_lanes(left, right):
+    return lax.dot_general(
+        left, right, (((1,), (1,)), ((), ())), preferred_element_type=jnp.float32
+    )
+
+
+def matmul(left, right):
+    return jnp.dot(left, right, preferred_element_type=jnp.float32)
+
+
+def split(value):
+    high = value.astype(jnp.bfloat16)
+    return high, (value - high.astype(jnp.float32)).astype(jnp.bfloat16)
+
+
+def exchange_kernel(
+    groups,
+    planes,
+    order_ref,
+    momentum_ref,
+    picked_ref,
+    rows_ref,
+    cols_ref,
+    twice_ref,
+    pairs_ref,
+    update_ref,
+    residual_ref,
+    box,
+    dense,
+    decoded,
+    send_sem,
+    recv_sem,
+):
+    spans = momentum_ref.shape[0]
+    entries = spans * TOPK
+    chunks = BLOCK * BLOCK // LANES
+    in_tile = LANES // TOPK
+    tiles = entries // LANES
+    devices = groups * planes
+    my_group, my_plane = lax.axis_index("grp"), lax.axis_index("rep")
+    group_of = [lax.rem(my_group + step, groups) for step in range(groups)]
+    plane_of = [lax.rem(my_plane + step, planes) for step in range(planes)]
+
+    def peer(plane, group):
+        return {"grp": group_of[group], "rep": plane_of[plane]}
+
+    others = [(z, g) for z in range(planes) for g in range(groups) if z or g]
+    barrier = pltpu.get_barrier_semaphore()
+    for z, g in others[::-1]:
+        pl.semaphore_signal(barrier, inc=1, device_id=peer(z, g), device_id_type=pl.DeviceIdType.MESH)
+
+    lane = lax.broadcasted_iota(jnp.int32, (spans, entries), 1)
+    mine = (lane // TOPK) == lax.broadcasted_iota(jnp.int32, (spans, entries), 0)
+    spread = jnp.concatenate([picked_ref[...]] * spans, axis=1)
+    spots = jnp.sum(jnp.where(mine, spread, 0), axis=0, keepdims=True)
+    freq = lax.broadcasted_iota(jnp.int32, (BLOCK, entries), 0)
+    one_row = jnp.where(freq == spots // BLOCK, 1.0, 0.0).astype(jnp.bfloat16)
+    one_col = jnp.where(freq == spots % BLOCK, 1.0, 0.0).astype(jnp.bfloat16)
+    half_rows = chunks * spans
+    wave = matmul(cols_ref[...], one_col).astype(jnp.bfloat16)
+    blank = jnp.zeros_like(wave)
+    waves = (jnp.concatenate([wave, blank], axis=0), jnp.concatenate([blank, wave], axis=0))
+    momentum = jnp.concatenate(
+        [momentum_ref[:, k * LANES : (k + 1) * LANES].astype(jnp.float32) for k in range(chunks)],
+        axis=0,
+    )
+    momentum_low = momentum.astype(jnp.bfloat16)
+    total = jnp.zeros((spans, entries), jnp.float32)
+    row_waves = []
+    for p in range(2):
+        row_wave = matmul(rows_ref[p * half_rows : (p + 1) * half_rows, :], one_row)
+        row_waves.append(row_wave)
+        product = row_wave * matmul(momentum_low, waves[p])
+        total += jnp.sum(product.reshape(chunks, spans, entries), axis=0)
+    chosen = jnp.sum(jnp.where(mine, total, 0.0), axis=0, keepdims=True)
+    chosen = chosen.astype(jnp.bfloat16).astype(jnp.float32)
+    box[0, 0:1, :] = chosen
+    box[0, 1:2, :] = spots.astype(jnp.float32)
+
+    pl.semaphore_wait(barrier, devices - 1)
+    copies = []
+    for z, g in others[::-1]:
+        copy = pltpu.make_async_remote_copy(
+            src_ref=box.at[0],
+            dst_ref=box.at[z * groups + g],
+            send_sem=send_sem,
+            recv_sem=recv_sem.at[z],
+            device_id=peer(z, g),
+            device_id_type=pl.DeviceIdType.MESH,
+        )
+        copy.start()
+        copies.append(copy)
+
+    correction = jnp.zeros((half_rows, LANES), jnp.float32)
+    scaled = jnp.where(mine, chosen, 0.0)
+    for p in range(2):
+        weight = row_waves[p].reshape(chunks, spans, entries) * scaled[None]
+        for part in split(weight.reshape(half_rows, entries)):
+            correction += contract_lanes(part, waves[p])
+    residual = momentum - correction
+    for k in range(chunks):
+        residual_ref[:, k * LANES : (k + 1) * LANES] = residual[
+            k * spans : (k + 1) * spans
+        ].astype(jnp.bfloat16)
+
+    offset = (lax.broadcasted_iota(jnp.int32, (1, LANES), 1) // TOPK) * BLOCK
+    tall = lax.broadcasted_iota(jnp.int32, (in_tile * BLOCK, LANES), 0)
+    short = lax.broadcasted_iota(jnp.int32, (BLOCK, LANES), 0)
+    sums = [jnp.zeros((in_tile * BLOCK, BLOCK), jnp.float32) for _ in range(tiles)]
+    reach = sorted(range(planes), key=lambda z: min(z, planes - z))
+    for z in reach:
+        first = 1 if z == 0 else 0
+        landed = box.at[pl.ds(z * groups + first, groups - first)]
+        pltpu.make_async_copy(landed, landed, recv_sem.at[z]).wait()
+        for h in range(tiles):
+            left, right = [], []
+            for g in range(groups):
+                slot = box[z * groups + g, :, h * LANES : (h + 1) * LANES]
+                value = slot[0:1]
+                spot = slot[1:2].astype(jnp.int32)
+                left.append(jnp.where(tall == spot // BLOCK + offset, 1.0, 0.0).astype(jnp.bfloat16))
+                right.append(jnp.where(short == spot % BLOCK, value, 0.0).astype(jnp.bfloat16))
+            sums[h] += contract_lanes(
+                jnp.concatenate(left, axis=1), jnp.concatenate(right, axis=1)
+            )
+    lower = lax.broadcasted_iota(jnp.int32, (BLOCK, LANES), 1) < BLOCK
+    for h in range(tiles):
+        half = sum(matmul(part, twice_ref[...]) for part in split(sums[h]))
+        for c in range(in_tile):
+            dense[h * in_tile + c] = half[c * BLOCK : (c + 1) * BLOCK]
+    for s in range(spans):
+        half = dense[order_ref[s]]
+        stacked = jnp.concatenate(
+            [jnp.where(lower, half, 0.0), jnp.where(lower, 0.0, half)], axis=0
+        )
+        decoded[pl.ds(s, chunks, stride=spans), :] = matmul(
+            pairs_ref[...], stacked.astype(jnp.bfloat16)
+        )
+    for k in range(chunks):
+        update_ref[:, k * LANES : (k + 1) * LANES] = decoded[
+            k * spans : (k + 1) * spans, :
+        ].astype(jnp.bfloat16)
+    for copy in copies:
+        copy.wait_send()
+
+
+def local_small(groups, planes, momentum, picked, owner_span_order):
+    spans = momentum.shape[0]
+    chunks = BLOCK * BLOCK // LANES
+    table = cosine_table()
+    by_pair = table.T.reshape(chunks, 2, BLOCK)
+    rows = np.repeat(by_pair.transpose(1, 0, 2), spans, axis=1).reshape(-1, BLOCK)
+    constants = [rows, table.T, np.concatenate([table, table], axis=1), by_pair.reshape(chunks, LANES)]
+    vmem = pl.BlockSpec(memory_space=pltpu.VMEM)
+    return pl.pallas_call(
+        functools.partial(exchange_kernel, groups, planes),
+        out_shape=(
+            jax.ShapeDtypeStruct(momentum.shape, jnp.bfloat16),
+            jax.ShapeDtypeStruct(momentum.shape, jnp.bfloat16),
+        ),
+        in_specs=[pl.BlockSpec(memory_space=pltpu.SMEM)] + [vmem] * 6,
+        out_specs=(vmem, vmem),
+        scratch_shapes=[
+            pltpu.VMEM((groups * planes, 2, spans * TOPK), jnp.float32),
+            pltpu.VMEM((spans, BLOCK, LANES), jnp.float32),
+            pltpu.VMEM((chunks * spans, LANES), jnp.float32),
+            pltpu.SemaphoreType.DMA,
+            pltpu.SemaphoreType.DMA((planes,)),
+        ],
+        compiler_params=pltpu.CompilerParams(collective_id=0, has_side_effects=True),
+    )(owner_span_order, momentum, picked, *[jnp.asarray(c, dtype=jnp.bfloat16) for c in constants])
+
+
+def local(groups, planes, momentum, picked, owner_span_order):
+    entries = momentum.shape[0] * TOPK
+    if entries % LANES == 0 and groups * planes * entries * 8 <= GATHER_BYTES:
+        return local_small(groups, planes, momentum, picked, owner_span_order)
+    return local_large(momentum, picked, owner_span_order)
+
+
 def solution(mesh):
     return jax.shard_map(
-        local,
+        functools.partial(local, mesh.shape["grp"], mesh.shape["rep"]),
         mesh=mesh,
         in_specs=(P(("grp", "rep"), None), P(("grp", "rep"), None), P()),
         out_specs=(P(), P(("grp", "rep"), None)),

time: 55.4 us -> 16.6 us (0.30)
  blocking collectives: 27.6 us -> 0 us
  Pallas kernels: 0 us -> 13.6 us
  starting transfers between devices: 8.52 us -> 0 us
  waiting for transfers between devices: 6.04 us -> 0 us
  local copies, waits for them, and re-layouts: 7.25 us -> 2.14 us
  other arithmetic: 3 us -> 0 us
  matrix products: 1.86 us -> 0 us
    psum x1 -> x0, blocking collectives: 19.4 us -> none  [local(): partial_sum = lax.psum(partial_sum, 'rep')]
    pallas_call x0 -> x1, Pallas kernels: none -> 13.6 us  [local_small(): pl.pallas_call(functools.partial(exchange_kernel, groups, planes), out_sh...]
    all_to_all x2 -> x0, starting transfers between devices: 8.52 us -> none  [the longest x1 5.21 us: local(): lax.all_to_all(shaped[0], 'grp', split_axis=0, concat_axis=2, tiled=True)]
    all_gather x1 -> x0, blocking collectives: 8.26 us -> none  [local(): update = lax.all_gather(my_share, 'grp', axis=0, tiled=True)]
    all_to_all x2 -> x0, waiting for transfers between devices: 6.04 us -> none  [the longest x1 3.79 us: local(): lax.all_to_all(shaped[1], 'grp', split_axis=0, concat_axis=2, tiled=True)]
    gather x5 -> x0, local copies, waits for them, and re-layouts: 3.68 us -> none  [the longest x3 2.56 us: local(): jnp.take_along_axis(transform_coefficients, picked, axis=1)]
    dot_general x7 -> x0, matrix products: 1.86 us -> none  [the longest x1 0.6 us: decode_sparse(): jnp.einsum('cij,jb->cib', square, cos_low, preferred_element_type=jnp.flo...]
    select_n x5 -> x0, other arithmetic: 0.77 us -> none  [the longest x1 0.66 us: local(): slot_spots = jnp.take(picked, owner_span_order, axis=0)]
  transfers between devices with their start and end apart: 2 -> 0, of which waited for: 2 -> 0; matrix products, arithmetic and copies ran while one was open for 6% -> 0% of each run, Pallas kernels for 0% -> 0%
where the time goes in v1:
time: 16.6 us; the launch traced here: 16.4 us
  Pallas kernels  13.6 us (82%)
  local copies, waits for them, and re-layouts  2.14 us (13%)
  between operations  0.65 us (4%)
    pallas_call x1, Pallas kernels, local_small(): pl.pallas_call(functools.partial(exchange_kernel, groups, planes), out_sh...  13.6 us
    unnamed x4, local copies, waits for them, and re-layouts  2.14 us

profile of v1, /device:TPU:0, one launch (start us, length us, event | category | flops | bytes accessed | tf_op | source)
XLA Modules:
  0.0 16.4 jit_solution(4326099134196122193)
XLA Ops:
  0.6 13.6 %shard_map.86 = (bf16[8,4096]{1,0:T(8,128)(2,1)}, bf16[8,4096]{1,0:T(8,128)(2,1)}) custom-call(s32[8]{0:T(128)} %order_ref.1, bf16[8,4096]{1,0:T(8,128)(2,1)} %momentum_ref.1, s32[8,32]{1,0:T(8,128)} %picked_ref.1, bf16[512,64]{1,0:T(8,128)(2,1)} %constant.8.clone.rows_ref, bf16[64,64]{1,0:T(8,128)(2,1)} %constant.9.clone.cols_ref, ...), custom_call_target="tpu_custom_call" | custom-call | tf_op jit(solution)/shard_map/pallas_call | solution.py:277
  14.3 0.0 copy-start
  14.3 1.5 %copy.11 = bf16[8,4096]{1,0:T(8,128)(2,1)} copy(bf16[8,4096]{1,0:T(8,128)(2,1)} %get-tuple-element.4) | data formatting | bytes 131072
  15.8 0.0 copy-done
  15.8 0.6 %copy.12 = bf16[8,4096]{1,0:T(8,128)(2,1)} copy(bf16[8,4096]{1,0:T(8,128)(2,1)S(1)} %copy-done) | data formatting | bytes 131072
Async XLA Ops:
  14.3 1.5 %copy-start = (bf16[8,4096]{1,0:T(8,128)(2,1)S(1)}, bf16[8,4096]{1,0:T(8,128)(2,1)}, u32[]{:S(2)}) copy-start(bf16[8,4096]{1,0:T(8,128)(2,1)} %get-tuple-element.5) | copy-start | bytes 196612

commit v2 on v1

--- a/solution.py
+++ b/solution.py
@@ -139,20 +139,37 @@
     groups,
     planes,
     order_ref,
+    momentum_hbm,
+    picked_hbm,
+    rows_hbm,
+    cols_hbm,
+    twice_hbm,
+    pairs_hbm,
+    update_ref,
+    residual_ref,
     momentum_ref,
     picked_ref,
     rows_ref,
     cols_ref,
     twice_ref,
     pairs_ref,
-    update_ref,
-    residual_ref,
-    box,
+    value_box,
+    spot_box,
     dense,
     decoded,
+    load_sem,
     send_sem,
-    recv_sem,
+    value_sem,
+    spot_sem,
 ):
+    sources = (picked_hbm, cols_hbm, rows_hbm, momentum_hbm, twice_hbm, pairs_hbm)
+    targets = (picked_ref, cols_ref, rows_ref, momentum_ref, twice_ref, pairs_ref)
+    loads = [
+        pltpu.make_async_copy(source, target, load_sem.at[n])
+        for n, (source, target) in enumerate(zip(sources, targets))
+    ]
+    for load in loads:
+        load.start()
     spans = momentum_ref.shape[0]
     entries = spans * TOPK
     chunks = BLOCK * BLOCK // LANES
@@ -171,6 +188,8 @@
     for z, g in others[::-1]:
         pl.semaphore_signal(barrier, inc=1, device_id=peer(z, g), device_id_type=pl.DeviceIdType.MESH)
 
+    for load in loads:
+        load.wait()
     lane = lax.broadcasted_iota(jnp.int32, (spans, entries), 1)
     mine = (lane // TOPK) == lax.broadcasted_iota(jnp.int32, (spans, entries), 0)
     spread = jnp.concatenate([picked_ref[...]] * spans, axis=1)
@@ -195,23 +214,31 @@
         product = row_wave * matmul(momentum_low, waves[p])
         total += jnp.sum(product.reshape(chunks, spans, entries), axis=0)
     chosen = jnp.sum(jnp.where(mine, total, 0.0), axis=0, keepdims=True)
-    chosen = chosen.astype(jnp.bfloat16).astype(jnp.float32)
-    box[0, 0:1, :] = chosen
-    box[0, 1:2, :] = spots.astype(jnp.float32)
+    chosen_low = chosen.astype(jnp.bfloat16)
+    chosen = chosen_low.astype(jnp.float32)
+
+    def by_tile(row):
+        return jnp.concatenate(
+            [row[:, h * LANES : (h + 1) * LANES] for h in range(tiles)], axis=0
+        )
+
+    value_box[0] = by_tile(chosen).astype(jnp.bfloat16)
+    spot_box[0] = by_tile(spots).astype(jnp.int16)
 
     pl.semaphore_wait(barrier, devices - 1)
     copies = []
     for z, g in others[::-1]:
-        copy = pltpu.make_async_remote_copy(
-            src_ref=box.at[0],
-            dst_ref=box.at[z * groups + g],
-            send_sem=send_sem,
-            recv_sem=recv_sem.at[z],
-            device_id=peer(z, g),
-            device_id_type=pl.DeviceIdType.MESH,
-        )
-        copy.start()
-        copies.append(copy)
+        for box, arrived in ((spot_box, spot_sem), (value_box, value_sem)):
+            copy = pltpu.make_async_remote_copy(
+                src_ref=box.at[0],
+                dst_ref=box.at[z * groups + g],
+                send_sem=send_sem,
+                recv_sem=arrived.at[z],
+                device_id=peer(z, g),
+                device_id_type=pl.DeviceIdType.MESH,
+            )
+            copy.start()
+            copies.append(copy)
 
     correction = jnp.zeros((half_rows, LANES), jnp.float32)
     scaled = jnp.where(mine, chosen, 0.0)
@@ -232,14 +259,16 @@
     reach = sorted(range(planes), key=lambda z: min(z, planes - z))
     for z in reach:
         first = 1 if z == 0 else 0
-        landed = box.at[pl.ds(z * groups + first, groups - first)]
-        pltpu.make_async_copy(landed, landed, recv_sem.at[z]).wait()
+        for box, arrived in ((spot_box, spot_sem), (value_box, value_sem)):
+            landed = box.at[pl.ds(z * groups + first, groups - first)]
+            pltpu.make_async_copy(landed, landed, arrived.at[z]).wait()
+        values = [value_box[z * groups + g].astype(jnp.float32) for g in range(groups)]
+        places = [spot_box[z * groups + g].astype(jnp.int32) for g in range(groups)]
         for h in range(tiles):
             left, right = [], []
             for g in range(groups):
-                slot = box[z * groups + g, :, h * LANES : (h + 1) * LANES]
-                value = slot[0:1]
-                spot = slot[1:2].astype(jnp.int32)
+                value = values[g][h : h + 1]
+                spot = places[g][h : h + 1]
                 left.append(jnp.where(tall == spot // BLOCK + offset, 1.0, 0.0).astype(jnp.bfloat16))
                 right.append(jnp.where(short == spot % BLOCK, value, 0.0).astype(jnp.bfloat16))
             sums[h] += contract_lanes(
@@ -266,6 +295,17 @@
         copy.wait_send()
 
 
+def store_kernel(update_ref, residual_ref, update_hbm, residual_hbm, sem):
+    stores = [
+        pltpu.make_async_copy(residual_ref, residual_hbm, sem.at[0]),
+        pltpu.make_async_copy(update_ref, update_hbm, sem.at[1]),
+    ]
+    for store in stores:
+        store.start()
+    for store in stores:
+        store.wait()
+
+
 def local_small(groups, planes, momentum, picked, owner_span_order):
     spans = momentum.shape[0]
     chunks = BLOCK * BLOCK // LANES
@@ -273,24 +313,37 @@
     by_pair = table.T.reshape(chunks, 2, BLOCK)
     rows = np.repeat(by_pair.transpose(1, 0, 2), spans, axis=1).reshape(-1, BLOCK)
     constants = [rows, table.T, np.concatenate([table, table], axis=1), by_pair.reshape(chunks, LANES)]
+    constants = [jnp.asarray(constant, dtype=jnp.bfloat16) for constant in constants]
+    operands = [momentum, picked, *constants]
+    anywhere = pl.BlockSpec(memory_space=pl.ANY)
     vmem = pl.BlockSpec(memory_space=pltpu.VMEM)
-    return pl.pallas_call(
+    devices = groups * planes
+    box_shape = (devices, spans * TOPK // LANES, LANES)
+    results = pl.pallas_call(
         functools.partial(exchange_kernel, groups, planes),
-        out_shape=(
-            jax.ShapeDtypeStruct(momentum.shape, jnp.bfloat16),
-            jax.ShapeDtypeStruct(momentum.shape, jnp.bfloat16),
-        ),
-        in_specs=[pl.BlockSpec(memory_space=pltpu.SMEM)] + [vmem] * 6,
-        out_specs=(vmem, vmem),
-        scratch_shapes=[
-            pltpu.VMEM((groups * planes, 2, spans * TOPK), jnp.float32),
+        out_shape=[pltpu.VMEM(momentum.shape, jnp.bfloat16)] * 2,
+        in_specs=[pl.BlockSpec(memory_space=pltpu.SMEM)] + [anywhere] * len(operands),
+        out_specs=[vmem] * 2,
+        scratch_shapes=[pltpu.VMEM(x.shape, x.dtype) for x in operands]
+        + [
+            pltpu.VMEM(box_shape, jnp.bfloat16),
+            pltpu.VMEM(box_shape, jnp.int16),
             pltpu.VMEM((spans, BLOCK, LANES), jnp.float32),
             pltpu.VMEM((chunks * spans, LANES), jnp.float32),
+            pltpu.SemaphoreType.DMA((len(operands),)),
             pltpu.SemaphoreType.DMA,
+            pltpu.SemaphoreType.DMA((planes,)),
             pltpu.SemaphoreType.DMA((planes,)),
         ],
         compiler_params=pltpu.CompilerParams(collective_id=0, has_side_effects=True),
-    )(owner_span_order, momentum, picked, *[jnp.asarray(c, dtype=jnp.bfloat16) for c in constants])
+    )(owner_span_order, *operands)
+    return pl.pallas_call(
+        store_kernel,
+        out_shape=[jax.ShapeDtypeStruct(momentum.shape, jnp.bfloat16)] * 2,
+        in_specs=[vmem] * 2,
+        out_specs=[anywhere] * 2,
+        scratch_shapes=[pltpu.SemaphoreType.DMA((2,))],
+    )(*[pltpu.with_memory_space_constraint(result, pltpu.VMEM) for result in results])
 
 
 def local(groups, planes, momentum, picked, owner_span_order):

time: 16.6 us -> 14.5 us (0.87)
  local copies, waits for them, and re-layouts: 2.14 us -> 0 us
    unnamed x4 -> x0, local copies, waits for them, and re-layouts: 2.14 us -> none
    pallas_call x0 -> x1, Pallas kernels: none -> 0.67 us  [local_small(): pl.pallas_call(store_kernel, out_shape=[jax.ShapeDtypeStruct(momentum.sha...]
    pallas_call x1, Pallas kernels: 13.6 us -> 13 us  [local_small(): pl.pallas_call(functools.partial(exchange_kernel, groups, planes), out_sh...]
where the time goes in v2:
time: 14.5 us; the launch traced here: 14.3 us
  Pallas kernels  13.7 us (94%)
  between operations  0.64 us (4%)
    pallas_call x1, Pallas kernels, local_small(): pl.pallas_call(functools.partial(exchange_kernel, groups, planes), out_sh...  13 us
    pallas_call x1, Pallas kernels, local_small(): pl.pallas_call(store_kernel, out_shape=[jax.ShapeDtypeStruct(momentum.sha...  0.67 us

profile of v2, /device:TPU:0, one launch (start us, length us, event | category | flops | bytes accessed | tf_op | source)
XLA Modules:
  0.0 14.3 jit_solution(12234058231658367484)
XLA Ops:
  0.6 13.0 %shard_map.86 = (bf16[8,4096]{1,0:T(8,128)(2,1)S(1)}, bf16[8,4096]{1,0:T(8,128)(2,1)S(1)}) custom-call(s32[8]{0:T(128)} %order_ref.1, bf16[8,4096]{1,0:T(8,128)(2,1)} %momentum_hbm.1, s32[8,32]{1,0:T(8,128)} %picked_hbm.1, bf16[512,64]{1,0:T(8,128)(2,1)} %constant.8.clone.rows_hbm, bf16[64,64]{1,0:T(8,128)(2,1)} %constant.9.clone.cols_hbm, ...), custom_call_target="tpu_custom_call" | custom-call | tf_op jit(solution)/shard_map/pallas_call | solution.py:322
  13.7 0.7 %shard_map.87 = (bf16[8,4096]{1,0:T(8,128)(2,1)}, bf16[8,4096]{1,0:T(8,128)(2,1)}) custom-call(bf16[8,4096]{1,0:T(8,128)(2,1)S(1)} %get-tuple-element.4.update_ref, bf16[8,4096]{1,0:T(8,128)(2,1)S(1)} %get-tuple-element.5.residual_ref), custom_call_target="tpu_custom_call" | custom-call | tf_op jit(solution)/shard_map/pallas_call | solution.py:340

commit v3 on v2

--- a/solution.py
+++ b/solution.py
@@ -138,7 +138,7 @@
 def exchange_kernel(
     groups,
     planes,
-    order_ref,
+    order_hbm,
     momentum_hbm,
     picked_hbm,
     rows_hbm,
@@ -147,6 +147,7 @@
     pairs_hbm,
     update_ref,
     residual_ref,
+    order_ref,
     momentum_ref,
     picked_ref,
     rows_ref,
@@ -162,14 +163,12 @@
     value_sem,
     spot_sem,
 ):
-    sources = (picked_hbm, cols_hbm, rows_hbm, momentum_hbm, twice_hbm, pairs_hbm)
-    targets = (picked_ref, cols_ref, rows_ref, momentum_ref, twice_ref, pairs_ref)
+    sources = (picked_hbm, cols_hbm, rows_hbm, momentum_hbm, twice_hbm, pairs_hbm, order_hbm)
+    targets = (picked_ref, cols_ref, rows_ref, momentum_ref, twice_ref, pairs_ref, order_ref)
     loads = [
         pltpu.make_async_copy(source, target, load_sem.at[n])
         for n, (source, target) in enumerate(zip(sources, targets))
     ]
-    for load in loads:
-        load.start()
     spans = momentum_ref.shape[0]
     entries = spans * TOPK
     chunks = BLOCK * BLOCK // LANES
@@ -188,6 +187,8 @@
     for z, g in others[::-1]:
         pl.semaphore_signal(barrier, inc=1, device_id=peer(z, g), device_id_type=pl.DeviceIdType.MESH)
 
+    for load in loads:
+        load.start()
     for load in loads:
         load.wait()
     lane = lax.broadcasted_iota(jnp.int32, (spans, entries), 1)
@@ -254,7 +255,13 @@
 
     offset = (lax.broadcasted_iota(jnp.int32, (1, LANES), 1) // TOPK) * BLOCK
     tall = lax.broadcasted_iota(jnp.int32, (in_tile * BLOCK, LANES), 0)
-    short = lax.broadcasted_iota(jnp.int32, (BLOCK, LANES), 0)
+    tall = tall.astype(jnp.float32).astype(jnp.bfloat16)
+    short = tall[:BLOCK]
+    one, zero = jnp.ones((), jnp.bfloat16), jnp.zeros((), jnp.bfloat16)
+
+    def low(integers):
+        return integers.astype(jnp.float32).astype(jnp.bfloat16)
+
     sums = [jnp.zeros((in_tile * BLOCK, BLOCK), jnp.float32) for _ in range(tiles)]
     reach = sorted(range(planes), key=lambda z: min(z, planes - z))
     for z in reach:
@@ -262,15 +269,15 @@
         for box, arrived in ((spot_box, spot_sem), (value_box, value_sem)):
             landed = box.at[pl.ds(z * groups + first, groups - first)]
             pltpu.make_async_copy(landed, landed, arrived.at[z]).wait()
-        values = [value_box[z * groups + g].astype(jnp.float32) for g in range(groups)]
+        values = [value_box[z * groups + g] for g in range(groups)]
         places = [spot_box[z * groups + g].astype(jnp.int32) for g in range(groups)]
         for h in range(tiles):
             left, right = [], []
             for g in range(groups):
                 value = values[g][h : h + 1]
                 spot = places[g][h : h + 1]
-                left.append(jnp.where(tall == spot // BLOCK + offset, 1.0, 0.0).astype(jnp.bfloat16))
-                right.append(jnp.where(short == spot % BLOCK, value, 0.0).astype(jnp.bfloat16))
+                left.append(jnp.where(tall == low(spot // BLOCK + offset), one, zero))
+                right.append(jnp.where(short == low(spot % BLOCK), value, zero))
             sums[h] += contract_lanes(
                 jnp.concatenate(left, axis=1), jnp.concatenate(right, axis=1)
             )
@@ -314,7 +321,7 @@
     rows = np.repeat(by_pair.transpose(1, 0, 2), spans, axis=1).reshape(-1, BLOCK)
     constants = [rows, table.T, np.concatenate([table, table], axis=1), by_pair.reshape(chunks, LANES)]
     constants = [jnp.asarray(constant, dtype=jnp.bfloat16) for constant in constants]
-    operands = [momentum, picked, *constants]
+    operands = [owner_span_order, momentum, picked, *constants]
     anywhere = pl.BlockSpec(memory_space=pl.ANY)
     vmem = pl.BlockSpec(memory_space=pltpu.VMEM)
     devices = groups * planes
@@ -322,9 +329,10 @@
     results = pl.pallas_call(
         functools.partial(exchange_kernel, groups, planes),
         out_shape=[pltpu.VMEM(momentum.shape, jnp.bfloat16)] * 2,
-        in_specs=[pl.BlockSpec(memory_space=pltpu.SMEM)] + [anywhere] * len(operands),
+        in_specs=[anywhere] * len(operands),
         out_specs=[vmem] * 2,
-        scratch_shapes=[pltpu.VMEM(x.shape, x.dtype) for x in operands]
+        scratch_shapes=[pltpu.SMEM(owner_span_order.shape, jnp.int32)]
+        + [pltpu.VMEM(x.shape, x.dtype) for x in operands[1:]]
         + [
             pltpu.VMEM(box_shape, jnp.bfloat16),
             pltpu.VMEM(box_shape, jnp.int16),
@@ -336,7 +344,7 @@
             pltpu.SemaphoreType.DMA((planes,)),
         ],
         compiler_params=pltpu.CompilerParams(collective_id=0, has_side_effects=True),
-    )(owner_span_order, *operands)
+    )(*operands)
     return pl.pallas_call(
         store_kernel,
         out_shape=[jax.ShapeDtypeStruct(momentum.shape, jnp.bfloat16)] * 2,

time: 14.5 us -> 14.1 us (0.972)
  Pallas kernels: 13.7 us -> 13.3 us
    pallas_call x1, Pallas kernels: 13 us -> 12.6 us  [local_small(): pl.pallas_call(functools.partial(exchange_kernel, groups, planes), out_sh...]
where the time goes in v3:
time: 14.1 us; the launch traced here: 13.9 us
  Pallas kernels  13.3 us (94%)
  between operations  0.64 us (5%)
    pallas_call x1, Pallas kernels, local_small(): pl.pallas_call(functools.partial(exchange_kernel, groups, planes), out_sh...  12.6 us
    pallas_call x1, Pallas kernels, local_small(): pl.pallas_call(store_kernel, out_shape=[jax.ShapeDtypeStruct(momentum.sha...  0.67 us

profile of v3, /device:TPU:0, one launch (start us, length us, event | category | flops | bytes accessed | tf_op | source)
XLA Modules:
  0.0 13.9 jit_solution(14688261818653602192)
XLA Ops:
  0.6 12.6 %shard_map.86 = (bf16[8,4096]{1,0:T(8,128)(2,1)S(1)}, bf16[8,4096]{1,0:T(8,128)(2,1)S(1)}) custom-call(s32[8]{0:T(128)} %order_hbm.1, bf16[8,4096]{1,0:T(8,128)(2,1)} %momentum_hbm.1, s32[8,32]{1,0:T(8,128)} %picked_hbm.1, bf16[512,64]{1,0:T(8,128)(2,1)} %constant.8.clone.rows_hbm, bf16[64,64]{1,0:T(8,128)(2,1)} %constant.9.clone.cols_hbm, ...), custom_call_target="tpu_custom_call" | custom-call | tf_op jit(solution)/shard_map/pallas_call | solution.py:329
  13.2 0.7 %shard_map.87 = (bf16[8,4096]{1,0:T(8,128)(2,1)}, bf16[8,4096]{1,0:T(8,128)(2,1)}) custom-call(bf16[8,4096]{1,0:T(8,128)(2,1)S(1)} %get-tuple-element.4.update_ref, bf16[8,4096]{1,0:T(8,128)(2,1)S(1)} %get-tuple-element.5.residual_ref), custom_call_target="tpu_custom_call" | custom-call | tf_op jit(solution)/shard_map/pallas_call | solution.py:348

commit v4 on v3

--- a/solution.py
+++ b/solution.py
@@ -156,6 +156,8 @@
     pairs_ref,
     value_box,
     spot_box,
+    turned_value,
+    turned_spot,
     dense,
     decoded,
     load_sem,
@@ -169,6 +171,8 @@
         pltpu.make_async_copy(source, target, load_sem.at[n])
         for n, (source, target) in enumerate(zip(sources, targets))
     ]
+    for load in loads:
+        load.start()
     spans = momentum_ref.shape[0]
     entries = spans * TOPK
     chunks = BLOCK * BLOCK // LANES
@@ -183,14 +187,12 @@
         return {"grp": group_of[group], "rep": plane_of[plane]}
 
     others = [(z, g) for z in range(planes) for g in range(groups) if z or g]
+    far_first = [o for o in others if o[0]] + [o for o in others if not o[0]]
     barrier = pltpu.get_barrier_semaphore()
-    for z, g in others[::-1]:
+    for z, g in far_first:
         pl.semaphore_signal(barrier, inc=1, device_id=peer(z, g), device_id_type=pl.DeviceIdType.MESH)
 
-    for load in loads:
-        load.start()
-    for load in loads:
-        load.wait()
+    loads[0].wait()
     lane = lax.broadcasted_iota(jnp.int32, (spans, entries), 1)
     mine = (lane // TOPK) == lax.broadcasted_iota(jnp.int32, (spans, entries), 0)
     spread = jnp.concatenate([picked_ref[...]] * spans, axis=1)
@@ -199,6 +201,8 @@
     one_row = jnp.where(freq == spots // BLOCK, 1.0, 0.0).astype(jnp.bfloat16)
     one_col = jnp.where(freq == spots % BLOCK, 1.0, 0.0).astype(jnp.bfloat16)
     half_rows = chunks * spans
+    for load in loads[1:]:
+        load.wait()
     wave = matmul(cols_ref[...], one_col).astype(jnp.bfloat16)
     blank = jnp.zeros_like(wave)
     waves = (jnp.concatenate([wave, blank], axis=0), jnp.concatenate([blank, wave], axis=0))
@@ -223,15 +227,22 @@
             [row[:, h * LANES : (h + 1) * LANES] for h in range(tiles)], axis=0
         )
 
-    value_box[0] = by_tile(chosen).astype(jnp.bfloat16)
-    spot_box[0] = by_tile(spots).astype(jnp.int16)
+    value_tile, spot_tile = by_tile(chosen), by_tile(spots)
+    value_box[0] = value_tile.astype(jnp.bfloat16)
+    spot_box[0] = spot_tile.astype(jnp.int16)
+    for turn in range(in_tile):
+        turned_value[turn] = pltpu.roll(value_tile, turn * TOPK, 1).astype(jnp.bfloat16)
+        turned_spot[turn] = pltpu.roll(spot_tile, turn * TOPK, 1).astype(jnp.int16)
 
     pl.semaphore_wait(barrier, devices - 1)
     copies = []
-    for z, g in others[::-1]:
-        for box, arrived in ((spot_box, spot_sem), (value_box, value_sem)):
+    for z, g in far_first:
+        for box, turned, arrived in (
+            (spot_box, turned_spot, spot_sem),
+            (value_box, turned_value, value_sem),
+        ):
             copy = pltpu.make_async_remote_copy(
-                src_ref=box.at[0],
+                src_ref=turned.at[g % in_tile],
                 dst_ref=box.at[z * groups + g],
                 send_sem=send_sem,
                 recv_sem=arrived.at[z],
@@ -241,58 +252,63 @@
             copy.start()
             copies.append(copy)
 
-    correction = jnp.zeros((half_rows, LANES), jnp.float32)
-    scaled = jnp.where(mine, chosen, 0.0)
-    for p in range(2):
-        weight = row_waves[p].reshape(chunks, spans, entries) * scaled[None]
-        for part in split(weight.reshape(half_rows, entries)):
-            correction += contract_lanes(part, waves[p])
-    residual = momentum - correction
-    for k in range(chunks):
-        residual_ref[:, k * LANES : (k + 1) * LANES] = residual[
-            k * spans : (k + 1) * spans
-        ].astype(jnp.bfloat16)
-
-    offset = (lax.broadcasted_iota(jnp.int32, (1, LANES), 1) // TOPK) * BLOCK
-    tall = lax.broadcasted_iota(jnp.int32, (in_tile * BLOCK, LANES), 0)
-    tall = tall.astype(jnp.float32).astype(jnp.bfloat16)
-    short = tall[:BLOCK]
+    def store_residual():
+        correction = jnp.zeros((half_rows, LANES), jnp.float32)
+        scaled = jnp.where(mine, chosen, 0.0)
+        for p in range(2):
+            weight = row_waves[p].reshape(chunks, spans, entries) * scaled[None]
+            for part in split(weight.reshape(half_rows, entries)):
+                correction += contract_lanes(part, waves[p])
+        residual = momentum - correction
+        for k in range(chunks):
+            residual_ref[:, k * LANES : (k + 1) * LANES] = residual[
+                k * spans : (k + 1) * spans
+            ].astype(jnp.bfloat16)
+
+    store_residual()
+    block = lax.broadcasted_iota(jnp.int32, (tiles, LANES), 1) // TOPK
+    taken = [block == turn for turn in range(in_tile)]
+    freq = lax.broadcasted_iota(jnp.int32, (BLOCK, groups * TOPK), 0)
+    freq = freq.astype(jnp.float32).astype(jnp.bfloat16)
     one, zero = jnp.ones((), jnp.bfloat16), jnp.zeros((), jnp.bfloat16)
 
     def low(integers):
         return integers.astype(jnp.float32).astype(jnp.bfloat16)
 
-    sums = [jnp.zeros((in_tile * BLOCK, BLOCK), jnp.float32) for _ in range(tiles)]
-    reach = sorted(range(planes), key=lambda z: min(z, planes - z))
-    for z in reach:
+    def span_rows(rows, c):
+        picks = []
+        for first in range(0, groups, in_tile):
+            row = rows[first]
+            for turn in range(1, in_tile):
+                row = jnp.where(taken[(c + turn) % in_tile], rows[first + turn], row)
+            picks.append(row)
+        return jnp.concatenate(picks, axis=1)
+
+    sums = [None] * spans
+    for z in range(planes):
         first = 1 if z == 0 else 0
         for box, arrived in ((spot_box, spot_sem), (value_box, value_sem)):
             landed = box.at[pl.ds(z * groups + first, groups - first)]
             pltpu.make_async_copy(landed, landed, arrived.at[z]).wait()
-        values = [value_box[z * groups + g] for g in range(groups)]
+        values = [value_box[z * groups + g].astype(jnp.float32) for g in range(groups)]
         places = [spot_box[z * groups + g].astype(jnp.int32) for g in range(groups)]
-        for h in range(tiles):
-            left, right = [], []
-            for g in range(groups):
-                value = values[g][h : h + 1]
-                spot = places[g][h : h + 1]
-                left.append(jnp.where(tall == low(spot // BLOCK + offset), one, zero))
-                right.append(jnp.where(short == low(spot % BLOCK), value, zero))
-            sums[h] += contract_lanes(
-                jnp.concatenate(left, axis=1), jnp.concatenate(right, axis=1)
-            )
-    lower = lax.broadcasted_iota(jnp.int32, (BLOCK, LANES), 1) < BLOCK
-    for h in range(tiles):
-        half = sum(matmul(part, twice_ref[...]) for part in split(sums[h]))
         for c in range(in_tile):
-            dense[h * in_tile + c] = half[c * BLOCK : (c + 1) * BLOCK]
+            value = span_rows(values, c).astype(jnp.bfloat16)
+            place = span_rows(places, c)
+            row, column = low(place // BLOCK), low(place % BLOCK)
+            for h in range(tiles):
+                left = jnp.where(freq == row[h : h + 1], one, zero)
+                right = jnp.where(freq == column[h : h + 1], value[h : h + 1], zero)
+                part = contract_lanes(left, right)
+                span = h * in_tile + c
+                sums[span] = part if z == 0 else sums[span] + part
+    for span in range(spans):
+        dense[span] = matmul(sums[span].astype(jnp.bfloat16), twice_ref[...])
+    lower = lax.broadcasted_iota(jnp.int32, (chunks, LANES), 1) < BLOCK
     for s in range(spans):
-        half = dense[order_ref[s]]
-        stacked = jnp.concatenate(
-            [jnp.where(lower, half, 0.0), jnp.where(lower, 0.0, half)], axis=0
-        )
-        decoded[pl.ds(s, chunks, stride=spans), :] = matmul(
-            pairs_ref[...], stacked.astype(jnp.bfloat16)
+        full = matmul(pairs_ref[...], dense[order_ref[s]].astype(jnp.bfloat16))
+        decoded[pl.ds(s, chunks, stride=spans), :] = jnp.where(
+            lower, full[:chunks], full[chunks:]
         )
     for k in range(chunks):
         update_ref[:, k * LANES : (k + 1) * LANES] = decoded[
@@ -319,12 +335,13 @@
     table = cosine_table()
     by_pair = table.T.reshape(chunks, 2, BLOCK)
     rows = np.repeat(by_pair.transpose(1, 0, 2), spans, axis=1).reshape(-1, BLOCK)
-    constants = [rows, table.T, np.concatenate([table, table], axis=1), by_pair.reshape(chunks, LANES)]
+    constants = [rows, table.T, np.concatenate([table, table], axis=1), by_pair.transpose(1, 0, 2).reshape(-1, BLOCK)]
     constants = [jnp.asarray(constant, dtype=jnp.bfloat16) for constant in constants]
     operands = [owner_span_order, momentum, picked, *constants]
     anywhere = pl.BlockSpec(memory_space=pl.ANY)
     vmem = pl.BlockSpec(memory_space=pltpu.VMEM)
     devices = groups * planes
+    turned_shape = (LANES // TOPK, spans * TOPK // LANES, LANES)
     box_shape = (devices, spans * TOPK // LANES, LANES)
     results = pl.pallas_call(
         functools.partial(exchange_kernel, groups, planes),
@@ -336,6 +353,8 @@
         + [
             pltpu.VMEM(box_shape, jnp.bfloat16),
             pltpu.VMEM(box_shape, jnp.int16),
+            pltpu.VMEM(turned_shape, jnp.bfloat16),
+            pltpu.VMEM(turned_shape, jnp.int16),
             pltpu.VMEM((spans, BLOCK, LANES), jnp.float32),
             pltpu.VMEM((chunks * spans, LANES), jnp.float32),
             pltpu.SemaphoreType.DMA((len(operands),)),
@@ -356,7 +375,7 @@
 
 def local(groups, planes, momentum, picked, owner_span_order):
     entries = momentum.shape[0] * TOPK
-    if entries % LANES == 0 and groups * planes * entries * 8 <= GATHER_BYTES:
+    if entries % LANES == 0 and groups % (LANES // TOPK) == 0 and groups * planes * entries * 8 <= GATHER_BYTES:
         return local_small(groups, planes, momentum, picked, owner_span_order)
     return local_large(momentum, picked, owner_span_order)
 

time: 14.1 us -> 12.9 us (0.915)
  Pallas kernels: 13.3 us -> 12.1 us
    pallas_call x1, Pallas kernels: 12.6 us -> 11.4 us  [local_small(): pl.pallas_call(functools.partial(exchange_kernel, groups, planes), out_sh...]
where the time goes in v4:
time: 12.9 us; the launch traced here: 12.8 us
  Pallas kernels  12.1 us (94%)
  between operations  0.64 us (5%)
    pallas_call x1, Pallas kernels, local_small(): pl.pallas_call(functools.partial(exchange_kernel, groups, planes), out_sh...  11.4 us
    pallas_call x1, Pallas kernels, local_small(): pl.pallas_call(store_kernel, out_shape=[jax.ShapeDtypeStruct(momentum.sha...  0.67 us

profile of v4, /device:TPU:0, one launch (start us, length us, event | category | flops | bytes accessed | tf_op | source)
XLA Modules:
  0.0 12.8 jit_solution(17733726795747001473)
XLA Ops:
  0.6 11.4 %shard_map.86 = (bf16[8,4096]{1,0:T(8,128)(2,1)S(1)}, bf16[8,4096]{1,0:T(8,128)(2,1)S(1)}) custom-call(s32[8]{0:T(128)} %order_hbm.1, bf16[8,4096]{1,0:T(8,128)(2,1)} %momentum_hbm.1, s32[8,32]{1,0:T(8,128)} %picked_hbm.1, bf16[512,64]{1,0:T(8,128)(2,1)} %constant.8.clone.rows_hbm, bf16[64,64]{1,0:T(8,128)(2,1)} %constant.9.clone.cols_hbm, ...), custom_call_target="tpu_custom_call" | custom-call | tf_op jit(solution)/shard_map/pallas_call | solution.py:346
  12.1 0.7 %shard_map.87 = (bf16[8,4096]{1,0:T(8,128)(2,1)}, bf16[8,4096]{1,0:T(8,128)(2,1)}) custom-call(bf16[8,4096]{1,0:T(8,128)(2,1)S(1)} %get-tuple-element.4.update_ref, bf16[8,4096]{1,0:T(8,128)(2,1)S(1)} %get-tuple-element.5.residual_ref), custom_call_target="tpu_custom_call" | custom-call | tf_op jit(solution)/shard_map/pallas_call | solution.py:367

commit v5 on v4

--- a/solution.py
+++ b/solution.py
@@ -154,16 +154,13 @@
     cols_ref,
     twice_ref,
     pairs_ref,
-    value_box,
-    spot_box,
-    turned_value,
-    turned_spot,
+    box,
+    turned,
     dense,
     decoded,
     load_sem,
     send_sem,
-    value_sem,
-    spot_sem,
+    recv_sem,
 ):
     sources = (picked_hbm, cols_hbm, rows_hbm, momentum_hbm, twice_hbm, pairs_hbm, order_hbm)
     targets = (picked_ref, cols_ref, rows_ref, momentum_ref, twice_ref, pairs_ref, order_ref)
@@ -198,8 +195,9 @@
     spread = jnp.concatenate([picked_ref[...]] * spans, axis=1)
     spots = jnp.sum(jnp.where(mine, spread, 0), axis=0, keepdims=True)
     freq = lax.broadcasted_iota(jnp.int32, (BLOCK, entries), 0)
-    one_row = jnp.where(freq == spots // BLOCK, 1.0, 0.0).astype(jnp.bfloat16)
-    one_col = jnp.where(freq == spots % BLOCK, 1.0, 0.0).astype(jnp.bfloat16)
+    row_spot, col_spot = spots // BLOCK, spots % BLOCK
+    one_row = jnp.where(freq == row_spot, 1.0, 0.0).astype(jnp.bfloat16)
+    one_col = jnp.where(freq == col_spot, 1.0, 0.0).astype(jnp.bfloat16)
     half_rows = chunks * spans
     for load in loads[1:]:
         load.wait()
@@ -226,31 +224,6 @@
         return jnp.concatenate(
             [row[:, h * LANES : (h + 1) * LANES] for h in range(tiles)], axis=0
         )
-
-    value_tile, spot_tile = by_tile(chosen), by_tile(spots)
-    value_box[0] = value_tile.astype(jnp.bfloat16)
-    spot_box[0] = spot_tile.astype(jnp.int16)
-    for turn in range(in_tile):
-        turned_value[turn] = pltpu.roll(value_tile, turn * TOPK, 1).astype(jnp.bfloat16)
-        turned_spot[turn] = pltpu.roll(spot_tile, turn * TOPK, 1).astype(jnp.int16)
-
-    pl.semaphore_wait(barrier, devices - 1)
-    copies = []
-    for z, g in far_first:
-        for box, turned, arrived in (
-            (spot_box, turned_spot, spot_sem),
-            (value_box, turned_value, value_sem),
-        ):
-            copy = pltpu.make_async_remote_copy(
-                src_ref=turned.at[g % in_tile],
-                dst_ref=box.at[z * groups + g],
-                send_sem=send_sem,
-                recv_sem=arrived.at[z],
-                device_id=peer(z, g),
-                device_id_type=pl.DeviceIdType.MESH,
-            )
-            copy.start()
-            copies.append(copy)
 
     def store_residual():
         correction = jnp.zeros((half_rows, LANES), jnp.float32)
@@ -265,15 +238,32 @@
                 k * spans : (k + 1) * spans
             ].astype(jnp.bfloat16)
 
-    store_residual()
+    parts = [by_tile(part) for part in (chosen, row_spot.astype(jnp.float32), col_spot.astype(jnp.float32))]
+    for turn in range(in_tile):
+        turned[turn] = jnp.concatenate(
+            [pltpu.roll(part, turn * TOPK, 1).astype(jnp.bfloat16) for part in parts], axis=1
+        )
+    box[0] = jnp.concatenate([part.astype(jnp.bfloat16) for part in parts], axis=1)
+    pl.when(my_plane == 0)(store_residual)
+    pl.semaphore_wait(barrier, devices - 1)
+    copies = []
+    for z, g in far_first:
+        copy = pltpu.make_async_remote_copy(
+            src_ref=turned.at[g % in_tile],
+            dst_ref=box.at[z * groups + g],
+            send_sem=send_sem,
+            recv_sem=recv_sem.at[z],
+            device_id=peer(z, g),
+            device_id_type=pl.DeviceIdType.MESH,
+        )
+        copy.start()
+        copies.append(copy)
+
     block = lax.broadcasted_iota(jnp.int32, (tiles, LANES), 1) // TOPK
     taken = [block == turn for turn in range(in_tile)]
     freq = lax.broadcasted_iota(jnp.int32, (BLOCK, groups * TOPK), 0)
     freq = freq.astype(jnp.float32).astype(jnp.bfloat16)
     one, zero = jnp.ones((), jnp.bfloat16), jnp.zeros((), jnp.bfloat16)
-
-    def low(integers):
-        return integers.astype(jnp.float32).astype(jnp.bfloat16)
 
     def span_rows(rows, c):
         picks = []
@@ -287,15 +277,16 @@
     sums = [None] * spans
     for z in range(planes):
         first = 1 if z == 0 else 0
-        for box, arrived in ((spot_box, spot_sem), (value_box, value_sem)):
-            landed = box.at[pl.ds(z * groups + first, groups - first)]
-            pltpu.make_async_copy(landed, landed, arrived.at[z]).wait()
-        values = [value_box[z * groups + g].astype(jnp.float32) for g in range(groups)]
-        places = [spot_box[z * groups + g].astype(jnp.int32) for g in range(groups)]
+        landed = box.at[pl.ds(z * groups + first, groups - first)]
+        pltpu.make_async_copy(landed, landed, recv_sem.at[z]).wait()
+        slots = [box[z * groups + g].astype(jnp.float32) for g in range(groups)]
+        values, rows, columns = (
+            [slot[:, n * LANES : (n + 1) * LANES] for slot in slots] for n in range(3)
+        )
         for c in range(in_tile):
-            value = span_rows(values, c).astype(jnp.bfloat16)
-            place = span_rows(places, c)
-            row, column = low(place // BLOCK), low(place % BLOCK)
+            value, row, column = (
+                span_rows(part, c).astype(jnp.bfloat16) for part in (values, rows, columns)
+            )
             for h in range(tiles):
                 left = jnp.where(freq == row[h : h + 1], one, zero)
                 right = jnp.where(freq == column[h : h + 1], value[h : h + 1], zero)
@@ -314,6 +305,7 @@
         update_ref[:, k * LANES : (k + 1) * LANES] = decoded[
             k * spans : (k + 1) * spans, :
         ].astype(jnp.bfloat16)
+    pl.when(my_plane != 0)(store_residual)
     for copy in copies:
         copy.wait_send()
 
@@ -341,8 +333,7 @@
     anywhere = pl.BlockSpec(memory_space=pl.ANY)
     vmem = pl.BlockSpec(memory_space=pltpu.VMEM)
     devices = groups * planes
-    turned_shape = (LANES // TOPK, spans * TOPK // LANES, LANES)
-    box_shape = (devices, spans * TOPK // LANES, LANES)
+    tile_shape = (spans * TOPK // LANES, 3 * LANES)
     results = pl.pallas_call(
         functools.partial(exchange_kernel, groups, planes),
         out_shape=[pltpu.VMEM(momentum.shape, jnp.bfloat16)] * 2,
@@ -351,15 +342,12 @@
         scratch_shapes=[pltpu.SMEM(owner_span_order.shape, jnp.int32)]
         + [pltpu.VMEM(x.shape, x.dtype) for x in operands[1:]]
         + [
-            pltpu.VMEM(box_shape, jnp.bfloat16),
-            pltpu.VMEM(box_shape, jnp.int16),
-            pltpu.VMEM(turned_shape, jnp.bfloat16),
-            pltpu.VMEM(turned_shape, jnp.int16),
+            pltpu.VMEM((devices, *tile_shape), jnp.bfloat16),
+            pltpu.VMEM((LANES // TOPK, *tile_shape), jnp.bfloat16),
             pltpu.VMEM((spans, BLOCK, LANES), jnp.float32),
             pltpu.VMEM((chunks * spans, LANES), jnp.float32),
             pltpu.SemaphoreType.DMA((len(operands),)),
             pltpu.SemaphoreType.DMA,
-            pltpu.SemaphoreType.DMA((planes,)),
             pltpu.SemaphoreType.DMA((planes,)),
         ],
         compiler_params=pltpu.CompilerParams(collective_id=0, has_side_effects=True),

time: 12.9 us -> 12.5 us (0.969)
  Pallas kernels: 12.1 us -> 11.6 us
    pallas_call x1, Pallas kernels: 11.4 us -> 11 us  [local_small(): pl.pallas_call(functools.partial(exchange_kernel, groups, planes), out_sh...]
where the time goes in v5:
time: 12.5 us; the launch traced here: 12.3 us
  Pallas kernels  11.6 us (93%)
  between operations  0.64 us (5%)
    pallas_call x1, Pallas kernels, local_small(): pl.pallas_call(functools.partial(exchange_kernel, groups, planes), out_sh...  11 us
    pallas_call x1, Pallas kernels, local_small(): pl.pallas_call(store_kernel, out_shape=[jax.ShapeDtypeStruct(momentum.sha...  0.67 us

profile of v5, /device:TPU:0, one launch (start us, length us, event | category | flops | bytes accessed | tf_op | source)
XLA Modules:
  0.0 12.3 jit_solution(9132161292089090562)
XLA Ops:
  0.6 11.0 %shard_map.86 = (bf16[8,4096]{1,0:T(8,128)(2,1)S(1)}, bf16[8,4096]{1,0:T(8,128)(2,1)S(1)}) custom-call(s32[8]{0:T(128)} %order_hbm.1, bf16[8,4096]{1,0:T(8,128)(2,1)} %momentum_hbm.1, s32[8,32]{1,0:T(8,128)} %picked_hbm.1, bf16[512,64]{1,0:T(8,128)(2,1)} %constant.8.clone.rows_hbm, bf16[64,64]{1,0:T(8,128)(2,1)} %constant.9.clone.cols_hbm, ...), custom_call_target="tpu_custom_call" | custom-call | tf_op jit(solution)/shard_map/pallas_call | solution.py:337
  11.6 0.7 %shard_map.87 = (bf16[8,4096]{1,0:T(8,128)(2,1)}, bf16[8,4096]{1,0:T(8,128)(2,1)}) custom-call(bf16[8,4096]{1,0:T(8,128)(2,1)S(1)} %get-tuple-element.4.update_ref, bf16[8,4096]{1,0:T(8,128)(2,1)S(1)} %get-tuple-element.5.residual_ref), custom_call_target="tpu_custom_call" | custom-call | tf_op jit(solution)/shard_map/pallas_call | solution.py:355
